TPU v7x, 32 devices: a whole 2x2x4 slice. The times are simulated.
32 devices in a mesh: row: 4 (over x, core), col: 8 (over z, y).
Axes of the slice: x: 2, y: 2, z: 4, core: 2. Of those that a mesh axis runs over, the one named last changes fastest.
Arguments:
- ancestor_inv: bfloat16 [32, 32, 256, 256], P('row', 'col'), may hold values from -0.29882812 to 0.29882812
- lower_panel: bfloat16 [8, 16, 256, 256], P('row', 'col'), may hold values from -0.59765625 to 0.59765625
- upper_panel: bfloat16 [8, 16, 256, 256], P('col', 'row'), may hold values from -0.59765625 to 0.59765625
- pivot_inv: float32 [8, 256, 256], P('col'), may hold values from -6 to 6
- members: int32 [8, 16], replicated, may hold values from -1 to 31, as said below
Outputs:
- lower_inv: bfloat16 [8, 16, 256, 256], P('col', 'row')
- upper_inv: bfloat16 [8, 16, 256, 256], P('row', 'col')
- diag_inv: float32 [8, 256, 256], P('col')
Inputs may be any that keep to these rules, and one draw needn't show every extreme that they name: `members`: slot s belongs to group g = s // 2; a used slot names an ancestor block of that group, from g * 4 to (g + 1) * 4 - 1. In each group of each supernode the used slots come first, name distinct blocks, and number 1 to 2; every group has 2 used slots for some supernode. Empty slots hold -1.
All inputs are finite; a program needn't handle non-finite values.
Results may differ from a plain program's by a relative error of at most 0.013.
Values may be sent and summed in bfloat16 or wider, within the bound.
A program may use at most 128 MiB of HBM per device.

v0:
```python
import jax
import jax.numpy as jnp
from jax import lax
from jax.sharding import PartitionSpec as P


def body(ancestor_inv, lower_panel, upper_panel, pivot_inv, members):
    n_col = lax.axis_size("col")
    n_row = lax.axis_size("row")
    row_index = lax.axis_index("row")
    col_index = lax.axis_index("col")
    row_blocks = ancestor_inv.shape[0]
    col_blocks = ancestor_inv.shape[1]
    side = ancestor_inv.shape[2]
    cap_slots = lower_panel.shape[1]
    row_slots = upper_panel.shape[1]
    level = members.shape[0]
    per_col = level // n_col
    zero_half = jnp.zeros((), jnp.bfloat16)
    row_members = lax.dynamic_slice_in_dim(members, row_index * row_slots, row_slots, 1)
    col_members = lax.dynamic_slice_in_dim(members, col_index * cap_slots, cap_slots, 1)
    row_valid = row_members >= 0
    col_valid = col_members >= 0
    row_local = jnp.clip(row_members - row_index * row_blocks, 0, row_blocks - 1)
    col_local = jnp.clip(col_members - col_index * col_blocks, 0, col_blocks - 1)
    flat_index = row_local[:, :, None] * col_blocks + col_local[:, None, :]
    block_pairs = jnp.take(
        ancestor_inv.reshape(row_blocks * col_blocks, side, side), flat_index, axis=0
    )
    pairs_here = block_pairs
    valid_here = row_valid
    masked = jnp.where(
        valid_here[:, :, None, None],
        lax.all_gather(upper_panel, "col", axis=0, tiled=True),
        zero_half,
    )
    upper_part = jnp.einsum(
        "kiab,kijbc->kjac", masked, pairs_here, preferred_element_type=jnp.float32
    )
    upper_part = jnp.where(col_valid[:, :, None, None], upper_part, 0.0)
    pairs_here = block_pairs
    valid_here = col_valid
    masked = jnp.where(
        valid_here[:, :, None, None],
        lax.all_gather(lower_panel, "row", axis=0, tiled=True),
        zero_half,
    )
    lower_part = jnp.einsum(
        "kijab,kjbc->kiac", pairs_here, masked, preferred_element_type=jnp.float32
    )
    lower_part = jnp.where(row_valid[:, :, None, None], lower_part, 0.0)
    lower_sum = lax.psum_scatter(lower_part, "col", scatter_dimension=0, tiled=True)
    lower_inv = (-lower_sum).astype(jnp.bfloat16)
    own_valid = lax.dynamic_slice_in_dim(row_valid, col_index * per_col, per_col, 0)
    own_upper = jnp.where(own_valid[:, :, None, None], upper_panel, zero_half)
    diag_part = jnp.einsum(
        "kiab,kibc->kac", own_upper, lower_inv, preferred_element_type=jnp.float32
    )
    band = side // n_row
    diag_stack = (
        diag_part.reshape(per_col, n_row, band, side)
        .transpose(1, 0, 2, 3)
        .reshape(n_row * per_col, band, side)
    )
    upper_sum, diag_band = (
        lax.psum_scatter(upper_part, "row", scatter_dimension=0, tiled=True),
        lax.psum_scatter(diag_stack, "row", scatter_dimension=0, tiled=True),
    )
    diag_sum = lax.all_gather(diag_band.astype(jnp.bfloat16), "row", axis=1, tiled=True).astype(
        diag_band.dtype
    )
    upper_inv = (-upper_sum).astype(jnp.bfloat16)
    diag_inv = pivot_inv - diag_sum
    return (lower_inv, upper_inv, diag_inv)


def solution(mesh):
    return jax.shard_map(
        body,
        mesh=mesh,
        in_specs=(
            P("row", "col", None, None),
            P("row", "col", None, None),
            P("col", "row", None, None),
            P("col", None, None),
            P(),
        ),
        out_specs=(P("col", "row", None, None), P("row", "col", None, None), P("col", None, None)),
        check_vma=False,
    )
```

profile of v0, /device:TPU:27, one launch (start us, length us, event | category | flops | bytes accessed | tf_op | source)
XLA Modules:
  0.0 339.9 jit_solution(1625667501854374602)
XLA Ops:
  7.2 0.0 all-gather.3.cloned.1.call-start
  7.2 0.7 all-gather.3.cloned.1.call-update
  7.9 0.0 all-gather.5.cloned.1.call-start
  7.9 0.7 all-gather.5.cloned.1.call-update
  8.6 0.0 reduce-scatter.4.cloned.1.call-start
  8.7 0.8 subtract_clamp_fusion
  9.5 0.8 clamp_multiply_fusion
  10.2 0.1 compare_select_fusion
  10.3 0.1 reshape.47
  10.5 7.8 %gather_fusion = bf16[64,256,256]{2,1,0:T(8,128)(2,1)} fusion(bf16[32,256,256]{2,1,0:T(8,128)(2,1)} %bitcast.46, s32[1024]{0:T(1024)S(1)} %pad_clamp_fusion), kind=kCustom, calls=%fused_computation | custom fusion | bytes 16777472 | tf_op jit(solution)/shard_map/jit(_take)/gather | solution.py:27
  18.2 0.1 dynamic-slice_compare_fusion
  18.3 0.1 dynamic-slice_compare_fusion.1
  18.4 0.1 fusion.18
  18.5 14.1 %all-gather.3.cloned.1.call-done = bf16[8,2,256,256]{3,2,1,0:T(8,128)(2,1)} async-done(((bf16[2,2,256,256]{3,2,1,0:T(8,128)(2,1)}), bf16[8,2,256,256]{3,2,1,0:T(8,128)(2,1)}) %all-gather.3.cloned.1.call-update) | async-done | bytes 2097168 | tf_op jit(solution)/shard_map/all_gather | solution.py:45
  32.6 9.6 %bitcast_select_fusion = f32[8,4,256,256]{3,2,1,0:T(8,128)} fusion(pred[8,4]{1,0:T(8,128)(4,1)S(1)} %dynamic-slice_compare_fusion.1, bf16[8,4,2,256,256]{4,3,2,1,0:T(8,128)(2,1)} %bitcast.47, pred[8,4,2]{2,1,0:T(4,128)(4,1)S(1)} %fusion.18, bf16[8,2,256,256]{3,2,1,0:T(8,128)(2,1)} %all-gather.3.cloned.1.call-done, pred[8,2]{1,0:T(8,128)(4,1)S(1)} %dynamic-slice_compare_fusion), kind=kOutput, calls=%fused_computation.1 | convolution fusion | flops 2154823680 | bytes 18874480 | tf_op jit(solution)/shard_map/kijab,kjbc->kiac/dot_general | solution.py:48
  42.2 0.0 reduce-scatter.4.cloned.1.call-update
  42.3 0.0 reduce-scatter.6.cloned.1.call-start
  42.3 64.2 %all-gather.5.cloned.1.call-done = bf16[8,4,256,256]{3,2,1,0:T(8,128)(2,1)} async-done(((bf16[1,4,256,256]{3,2,1,0:T(8,128)(2,1)}), bf16[8,4,256,256]{3,2,1,0:T(8,128)(2,1)}) %all-gather.5.cloned.1.call-update) | async-done | bytes 4194320 | tf_op jit(solution)/shard_map/all_gather | solution.py:34
  106.5 9.7 %fusion.2 = f32[8,2,256,256]{2,3,1,0:T(8,128)} fusion(pred[8,2]{1,0:T(8,128)(4,1)S(1)} %dynamic-slice_compare_fusion, bf16[8,4,256,256]{3,2,1,0:T(8,128)(2,1)} %all-gather.5.cloned.1.call-done, pred[8,4]{1,0:T(8,128)(4,1)S(1)} %dynamic-slice_compare_fusion.1, bf16[8,4,2,256,256]{4,3,2,1,0:T(8,128)(2,1)} %bitcast.48, pred[8,4,2]{2,1,0:T(4,128)(4,1)S(1)} %fusion.18), kind=kOutput, calls=%fused_computation.6 | convolution fusion | flops 2154823680 | bytes 16777328 | tf_op jit(solution)/shard_map/kiab,kijbc->kjac/dot_general | solution.py:37
  116.3 0.0 reduce-scatter.8.cloned.1.call-start
  116.3 0.9 copy-done.1
  117.3 0.1 broadcast_select_fusion.7
  117.4 138.7 %reduce-scatter.4.cloned.1.call-done = f32[1,4,256,256]{3,2,1,0:T(8,128)} async-done(((f32[8,4,256,256]{3,2,1,0:T(8,128)}), f32[1,4,256,256]{3,2,1,0:T(8,128)}) %reduce-scatter.4.cloned.1.call-update) | async-done | bytes 1048592 | tf_op jit(solution)/shard_map/reduce_scatter | solution.py:52
  256.1 1.3 negate_convert_fusion.1
  257.4 1.0 convolution_bitcast_fusion
  258.5 44.3 %reduce-scatter.6.cloned.1.call-done = f32[2,2,256,256]{2,3,1,0:T(8,128)} async-done(((f32[8,2,256,256]{2,3,1,0:T(8,128)}), f32[2,2,256,256]{2,3,1,0:T(8,128)}) %reduce-scatter.6.cloned.1.call-update) | async-done | bytes 1048592 | tf_op jit(solution)/shard_map/reduce_scatter | solution.py:66
  302.8 1.3 negate_convert_fusion
  304.1 1.0 copy.15
  305.1 20.6 %reduce-scatter.8.cloned.1.call-done = f32[1,64,256]{2,1,0:T(8,128)} async-done(((f32[4,64,256]{2,1,0:T(8,128)}), f32[1,64,256]{2,1,0:T(8,128)}) %reduce-scatter.8.cloned.1.call-update) | async-done | bytes 65552 | tf_op jit(solution)/shard_map/reduce_scatter | solution.py:67
  325.7 0.8 convert_element_type.14
  326.5 6.2 %all_gather.11 = bf16[1,256,256]{2,1,0:T(8,128)(2,1)S(1)} all-gather(bf16[1,64,256]{2,1,0:T(8,128)(2,1)S(1)} %convert_element_type.14), channel_id=1, replica_groups=mesh['row'=4,'col'=8] {'row'}, dimensions={1}, use_global_device_ids=true | all-gather | bytes 163840 | tf_op jit(solution)/shard_map/all_gather | solution.py:69
  332.7 0.7 convert_subtract_fusion
  (11 shorter events, 0.1 us)
Async XLA Ops:
  7.2 25.5 %all-gather.3.cloned.1.call-start = ((), (), s32[]{:S(2)}) async-start(), calls=%async_computation.3 | async-start | bytes 2621440 | tf_op jit(solution)/shard_map/all_gather | solution.py:45
  7.9 98.6 %all-gather.5.cloned.1.call-start = ((), (), s32[]{:S(2)}) async-start(), calls=%async_computation.5 | async-start | bytes 4718592 | tf_op jit(solution)/shard_map/all_gather | solution.py:34
  8.6 247.5 %reduce-scatter.4.cloned.1.call-start = ((), (), s32[]{:S(2)}) async-start(), calls=%async_computation.4 | async-start | bytes 9437184 | tf_op jit(solution)/shard_map/reduce_scatter | solution.py:52
  10.4 7.8 %copy-start.3 = (s32[8,16]{1,0:T(8,128)S(1)}, s32[8,16]{1,0:T(8,128)}, u32[]{:S(2)}) copy-start(s32[8,16]{1,0:T(8,128)} %param.9) | copy-start | bytes 1540
  42.3 260.5 %reduce-scatter.6.cloned.1.call-start = ((), (), s32[]{:S(2)}) async-start(), calls=%async_computation.6 | async-start | bytes 5242880 | tf_op jit(solution)/shard_map/reduce_scatter | solution.py:66
  116.2 1.0 copy-start.1
  116.3 216.4 %copy-start.2 = (f32[1,256,256]{2,1,0:T(8,128)S(1)}, f32[1,256,256]{2,1,0:T(8,128)}, u32[]{:S(2)}) copy-start(f32[1,256,256]{2,1,0:T(8,128)} %param.8) | copy-start | bytes 786436
  116.3 209.4 %reduce-scatter.8.cloned.1.call-start = ((), (), s32[]{:S(2)}) async-start(), calls=%async_computation.7 | async-start | bytes 327680 | tf_op jit(solution)/shard_map/reduce_scatter | solution.py:67
  257.4 76.0 %copy-start = (bf16[1,4,256,256]{3,2,1,0:T(8,128)(2,1)}, bf16[1,4,256,256]{3,2,1,0:T(8,128)(2,1)S(1)}, u32[]{:S(2)}) copy-start(bf16[1,4,256,256]{3,2,1,0:T(8,128)(2,1)S(1)} %negate_convert_fusion.1) | copy-start | bytes 1572868
Sparse Core Ops, SparseCore 0:
  9.5 23.0 all-gather.2
  34.7 71.7 all-gather.4
  110.2 145.9 reduce-scatter.3
  258.5 44.2 reduce-scatter.5
  305.7 19.9 reduce-scatter.7
where the time goes:
time: 342 us; the launch traced here: 340 us
  waiting for transfers between devices  283 us (83%)
  matrix products  20.3 us (6%)
  between operations  13.9 us (4%)
  local copies, waits for them, and re-layouts  9.86 us (3%)
  other arithmetic  6.15 us (2%)
  blocking collectives  6.15 us (2%)
    reduce_scatter x1, waiting for transfers between devices, body(): lax.psum_scatter(lower_part, 'col', scatter_dimension=0, tiled=True)  139 us
    all_gather x1, waiting for transfers between devices, body(): lax.all_gather(upper_panel, 'col', axis=0, tiled=True)  64.2 us
    reduce_scatter x1, waiting for transfers between devices, body(): lax.psum_scatter(upper_part, 'row', scatter_dimension=0, tiled=True)  44.3 us
    reduce_scatter x1, waiting for transfers between devices, body(): lax.psum_scatter(diag_stack, 'row', scatter_dimension=0, tiled=True)  20.6 us
    all_gather x1, waiting for transfers between devices, body(): lax.all_gather(lower_panel, 'row', axis=0, tiled=True)  14.1 us
    dot_general x1, matrix products, body(): jnp.einsum('kiab,kijbc->kjac', masked, pairs_here, preferred_element_type...  9.72 us
    dot_general x1, matrix products, body(): jnp.einsum('kijab,kjbc->kiac', pairs_here, masked, preferred_element_type...  9.62 us
    gather x1, local copies, waits for them, and re-layouts, body(): jnp.take(ancestor_inv.reshape(row_blocks * col_blocks, side, side), flat_...  7.78 us
  transfers between devices with their start and end apart: 5, of which 5 were waited for; matrix products, arithmetic and copies ran while one was open for 10% of the time, Pallas kernels for 0%

commit v1 on v0

v1 whole, which is shorter than its diff:
```python
import functools

import jax
import jax.numpy as jnp
from jax import lax
from jax.experimental import pallas as pl
from jax.experimental.pallas import tpu as pltpu
from jax.sharding import PartitionSpec as P

NY = 2
CORES = 2
BF = jnp.bfloat16
F32 = jnp.float32


def kernel(
    n_row, n_col, nq, hp,
    mem, anc, low, upp, piv,
    low_out, upp_out, diag_out,
    a, lbuf, ubuf, pl_buf, yr, zr, pu, ur, ds, dr, acc, dacc,
    loc, l_s, l_rel, l_r, uy_s, uy_r, uz_s, uz_r, ry_s, ry_r, rz_s, rz_r, pu_s, pu_r, d_s, d_r,
):
    row = lax.axis_index("row")
    col = lax.axis_index("col")
    nz = n_col // NY
    nx = n_row // CORES
    x, core = row // CORES, row % CORES
    z, y = col // NY, col % NY
    yp = z * NY + (1 - y)
    rb, cb = anc.shape[0], anc.shape[1]
    kr, cs = low.shape[0], low.shape[1]
    rs = upp.shape[1]
    ny_blocks = rs - nq
    hb = rs // hp
    partner = x * CORES + (1 - core)

    def remote(src, dst, ss, rsem, **where):
        return pltpu.make_async_remote_copy(
            src_ref=src, dst_ref=dst, send_sem=ss, recv_sem=rsem, device_id=where
        )

    ca = pltpu.make_async_copy(anc, a, loc.at[0])
    cl = pltpu.make_async_copy(low, lbuf.at[pl.ds(row * kr, kr)], loc.at[1])
    cu = pltpu.make_async_copy(upp.at[0], ubuf.at[col], loc.at[2])
    cl.start()
    cu.start()
    ca.start()

    bar = pltpu.get_barrier_semaphore()
    for dx in range(1, n_row):
        pl.semaphore_signal(bar, inc=1, device_id={"row": (row + dx) % n_row})
    pl.semaphore_signal(bar, inc=1, device_id={"col": yp})

    @pl.when(z > 0)
    def _():
        pl.semaphore_signal(bar, inc=1, device_id={"col": col - NY})

    @pl.when(z < nz - 1)
    def _():
        pl.semaphore_signal(bar, inc=1, device_id={"col": col + NY})

    peers = n_row + jnp.where(z > 0, 1, 0) + jnp.where(z < nz - 1, 1, 0)
    pl.semaphore_wait(bar, peers)

    def l_own(r2):
        return remote(low, lbuf.at[pl.ds(row * kr, kr)], l_s.at[r2], l_r.at[row], row=r2)

    def l_recv(r2):
        blk = lbuf.at[pl.ds(r2 * kr, kr)]
        return remote(blk, blk, l_rel.at[r2], l_r.at[r2], row=partner)

    def uy_own(kind):
        part = pl.ds(0, ny_blocks) if kind else pl.ds(ny_blocks, nq)
        return remote(
            upp.at[0, part], ubuf.at[col, part], uy_s.at[nz if kind == 0 else z],
            uy_r.at[nz if kind == 0 else z], col=yp,
        )

    def uy_got(kind, zs):
        part = pl.ds(0, ny_blocks) if kind else pl.ds(ny_blocks, nq)
        blk = ubuf.at[zs * NY + (1 - y), part]
        return remote(blk, blk, uy_s.at[zs], uy_r.at[nz if kind == 0 else zs], col=yp)

    def uy_pass(zs):
        blk = ubuf.at[zs * NY + y, pl.ds(0, ny_blocks)]
        return remote(blk, blk, uy_s.at[zs], uy_r.at[zs], col=yp)

    def uz(zs, kind, up):
        if kind == 0:
            blk = ubuf.at[zs * NY + y]
        else:
            blk = ubuf.at[zs * NY + (1 - y), pl.ds(ny_blocks, nq)]
        to = col + NY if up else col - NY
        return remote(blk, blk, uz_s.at[zs, int(up), kind], uz_r.at[zs, kind], col=to)

    def uz_own(up):
        to = col + NY if up else col - NY
        return remote(upp.at[0], ubuf.at[col], uz_s.at[z, int(up), 0], uz_r.at[z, 0], col=to)

    def ry(zd, h):
        part = pl.ds(h * hb, hb)
        return remote(
            pl_buf.at[zd * NY + (1 - y), part], yr.at[zd, part], ry_s.at[zd, h], ry_r.at[zd, h],
            col=yp,
        )

    def rz(zd, h, up):
        part = pl.ds(h * hb, hb)
        slot = zd + 1 if up else zd
        to = col + NY if up else col - NY
        return remote(
            pl_buf.at[zd * NY + y, part], zr.at[slot, part], rz_s.at[zd, h], rz_r.at[slot, h],
            col=to,
        )

    def pu_copy(k):
        return remote(pu.at[k], ur.at[row, k % kr], pu_s.at[k], pu_r.at[row, k % kr], row=k // kr)

    def pu_got(r2, p):
        return remote(pu.at[0], ur.at[r2, p], pu_s.at[0], pu_r.at[r2, p], row=r2)

    def d_copy(r2):
        return remote(ds, dr.at[row], d_s.at[r2], d_r.at[row], row=r2)

    def d_got(r2):
        return remote(ds, dr.at[r2], d_s.at[r2], d_r.at[r2], row=r2)

    def each_dir(fn):
        @pl.when(z > 0)
        def _():
            fn(False)

        @pl.when(z < nz - 1)
        def _():
            fn(True)

    def row_member(k, i):
        m = mem[k, row * rs + i]
        return m >= 0, jnp.clip(m - row * rb, 0, rb - 1)

    def col_member(k, j):
        m = mem[k, col * cs + j]
        return m >= 0, jnp.clip(m - col * cb, 0, cb - 1)

    zero = jnp.zeros((), BF)

    def lower_part(k):
        cols = [col_member(k, j) for j in range(cs)]
        panels = [jnp.where(cols[j][0], lbuf[k, j], zero) for j in range(cs)]

        def one(i, _):
            ok, ri = row_member(k, i)
            tot = None
            for j in range(cs):
                t = jnp.dot(a[ri, cols[j][1]], panels[j], preferred_element_type=F32)
                tot = t if tot is None else tot + t
            pl_buf[k, i] = jnp.where(ok, tot, 0.0).astype(BF)
            return 0

        lax.fori_loop(0, rs, one, 0)

    def upper_part(k):
        rows = [row_member(k, i) for i in range(rs)]

        def one(j, _):
            ok, cj = col_member(k, j)
            tot = None
            for i in range(rs):
                t = jnp.dot(
                    jnp.where(rows[i][0], ubuf[k, i], zero), a[rows[i][1], cj],
                    preferred_element_type=F32,
                )
                tot = t if tot is None else tot + t
            pu[k, j] = jnp.where(ok, tot, 0.0).astype(BF)
            return 0

        lax.fori_loop(0, cs, one, 0)

        @pl.when(k // kr != row)
        def _():
            pu_copy(k).start()

    def lower_group(r2):
        def one(p, _):
            k = r2 * kr + (p + 1 - y) % NY
            lower_part(k)

            @pl.when(k % NY != y)
            def _():
                for h in range(hp):
                    ry(k // NY, h).start()

            return 0

        lax.fori_loop(0, kr, one, 0)

    l_own(partner).start()
    for dx in range(1, nx):
        l_own(((x + dx) % nx) * CORES + core).start()
    uy_own(0).start()
    each_dir(lambda up: uz_own(up).start())

    ca.wait()
    cl.wait()
    lower_group(row)
    l_recv(partner).wait_recv()
    lower_group(partner)

    uy_got(0, z).wait_recv()
    each_dir(lambda up: uz(z, 1, up).start())
    cu.wait()
    upper_part(col)

    def others(fn):
        for dx in range(1, nx):
            fn((x + dx) % nx)

    def relay(x2):
        l_recv(x2 * CORES + core).wait_recv()
        l_recv(x2 * CORES + core).start()

    others(relay)

    def by_side(d, fn):
        @pl.when(z - d >= 0)
        def _():
            fn(z - d, True)

        @pl.when(z + d <= nz - 1)
        def _():
            fn(z + d, False)

    def take(zs, up):
        for kind in range(2):
            uz(zs, kind, up).wait_recv()

            @pl.when((z < nz - 1) if up else (z > 0))
            def _():
                uz(zs, kind, up).start()

    by_side(1, take)

    def late(x2):
        lower_group(x2 * CORES + core)
        l_recv(x2 * CORES + 1 - core).wait_recv()
        lower_group(x2 * CORES + 1 - core)

    others(late)
    uy_own(1).start()
    by_side(1, lambda zs, up: uy_pass(zs).start())

    def near(d):
        def one(s, _):
            zs = z + (2 * s - 1) * d

            @pl.when(jnp.logical_and(zs >= 0, zs < nz))
            def _():
                upper_part(zs * NY + y)

            return 0

        lax.fori_loop(0, 2, one, 0)

    def far(d):
        def one(s, _):
            zs = z + (2 * s - 1) * d

            @pl.when(jnp.logical_and(zs >= 0, zs < nz))
            def _():
                uy_got(1, zs).wait_recv()
                upper_part(zs * NY + (1 - y))

            return 0

        lax.fori_loop(0, 2, one, 0)

    def band_sum(zd, t):
        k = zd * NY + y

        def go(up):
            def piece(h, _):
                part = pl.ds(h * hb, hb)
                ry(zd, h).wait_recv()

                @pl.when((z > 0) if up else (z < nz - 1))
                def _():
                    rz(zd, h, up).wait_recv()
                    slot = zd + 1 if up else zd
                    pl_buf[k, part] = (
                        pl_buf[k, part].astype(F32) + yr[zd, part].astype(F32)
                        + zr[slot, part].astype(F32)
                    ).astype(BF)

                @pl.when((z == 0) if up else (z == nz - 1))
                def _():
                    pl_buf[k, part] = (
                        pl_buf[k, part].astype(F32) + yr[zd, part].astype(F32)
                    ).astype(BF)

                rz(zd, h, up).start()
                return 0

            lax.fori_loop(0, hp, piece, 0)

        @pl.when(zd > z)
        def _():
            go(True)

        @pl.when(zd < z)
        def _():
            go(False)

    def chain(t):
        band_sum((CORES * x + t) % nz, t)

    near(1)
    chain(0)
    for d in range(2, nz):
        by_side(d, take)
        by_side(d, lambda zs, up: uy_pass(zs).start())
        near(d)
        chain(d - 1)
    uy_got(1, z).wait_recv()
    upper_part(yp)
    far(1)
    chain(nz - 1)

    def final(h, _):
        part = pl.ds(h * hb, hb)
        ry(z, h).wait_recv()
        acc[part] = pl_buf[col, part].astype(F32) + yr[z, part].astype(F32)

        @pl.when(z > 0)
        def _():
            rz(z, h, True).wait_recv()
            acc[part] = acc[part] + zr[z + 1, part].astype(F32)

        @pl.when(z < nz - 1)
        def _():
            rz(z, h, False).wait_recv()
            acc[part] = acc[part] + zr[z, part].astype(F32)

        low_out[0, part] = (-acc[part]).astype(BF)
        return 0

    lax.fori_loop(0, hp, final, 0)
    tot = None
    for i in range(rs):
        t = jnp.dot(
            jnp.where(row_member(col, i)[0], ubuf[col, i], zero), low_out[0, i],
            preferred_element_type=F32,
        )
        tot = t if tot is None else tot + t
    dacc[...] = tot
    ds[...] = tot.astype(BF)
    for dx in range(1, n_row):
        d_copy((row + dx) % n_row).start()

    lax.fori_loop(2, nz, lambda d, _: (far(d), 0)[1], 0)

    for dx in range(1, n_row):
        r2 = (row + dx) % n_row
        d_got(r2).wait_recv()
        dacc[...] = dacc[...] + dr[r2].astype(F32)
    diag_out[0] = piv[0] - dacc[...]

    for p in range(kr):
        for j in range(cs):
            acc[p * cs + j] = pu[row * kr + p, j].astype(F32)
    for dx in range(1, n_row):
        r2 = (row + dx) % n_row
        for p in range(kr):
            pu_got(r2, p).wait_recv()
            for j in range(cs):
                acc[p * cs + j] = acc[p * cs + j] + ur[r2, p, j].astype(F32)
    for p in range(kr):
        for j in range(cs):
            upp_out[p, j] = (-acc[p * cs + j]).astype(BF)

    l_own(partner).wait_send()
    for dx in range(1, nx):
        r2 = ((x + dx) % nx) * CORES + core
        l_own(r2).wait_send()
        l_recv(r2).wait_send()
    uy_own(0).wait_send()
    uy_own(1).wait_send()

    def own_done(up):
        uz_own(up).wait_send()
        uz(z, 1, up).wait_send()

    each_dir(own_done)

    def passed(zs, up):
        uy_pass(zs).wait_send()

        @pl.when((z < nz - 1) if up else (z > 0))
        def _():
            for kind in range(2):
                uz(zs, kind, up).wait_send()

    for d in range(1, nz):
        by_side(d, passed)

    def sums_done(zd, _):
        for h in range(hp):
            ry(zd, h).wait_send()

            @pl.when(zd > z)
            def _():
                rz(zd, h, True).wait_send()

            @pl.when(zd < z)
            def _():
                rz(zd, h, False).wait_send()

        return 0

    lax.fori_loop(0, nz, sums_done, 0)

    def parts_done(k, _):
        @pl.when(k // kr != row)
        def _():
            pu_copy(k).wait_send()

        return 0

    lax.fori_loop(0, n_col, parts_done, 0)
    for dx in range(1, n_row):
        d_copy((row + dx) % n_row).wait_send()


def body(ancestor_inv, lower_panel, upper_panel, pivot_inv, members):
    n_col = lax.axis_size("col")
    n_row = lax.axis_size("row")
    side = ancestor_inv.shape[2]
    rb, cb = ancestor_inv.shape[:2]
    kr, cs = lower_panel.shape[:2]
    per_col, rs = upper_panel.shape[:2]
    level = members.shape[0]
    nz = n_col // NY
    assert per_col == 1 and level == n_col and kr == NY and nz == n_row
    hp = 2
    nq = rs // 4
    blk = (side, side)
    dma = pltpu.SemaphoreType.DMA
    vmem = pl.BlockSpec(memory_space=pltpu.VMEM)
    hbm = pl.BlockSpec(memory_space=pltpu.HBM)
    return pl.pallas_call(
        functools.partial(kernel, n_row, n_col, nq, hp),
        out_shape=(
            jax.ShapeDtypeStruct((per_col, rs) + blk, BF),
            jax.ShapeDtypeStruct((kr, cs) + blk, BF),
            jax.ShapeDtypeStruct((per_col,) + blk, F32),
        ),
        in_specs=[pl.BlockSpec(memory_space=pltpu.SMEM), hbm, hbm, hbm, vmem],
        out_specs=(vmem, vmem, vmem),
        scratch_shapes=[
            pltpu.VMEM((rb, cb) + blk, BF),
            pltpu.VMEM((level, cs) + blk, BF),
            pltpu.VMEM((n_col, rs) + blk, BF),
            pltpu.VMEM((n_col, rs) + blk, BF),
            pltpu.VMEM((nz, rs) + blk, BF),
            pltpu.VMEM((nz + 1, rs) + blk, BF),
            pltpu.VMEM((level, cs) + blk, BF),
            pltpu.VMEM((n_row, kr, cs) + blk, BF),
            pltpu.VMEM(blk, BF),
            pltpu.VMEM((n_row,) + blk, BF),
            pltpu.VMEM((max(rs, kr * cs),) + blk, F32),
            pltpu.VMEM(blk, F32),
            dma((3,)), dma((n_row,)), dma((n_row,)), dma((n_row,)),
            dma((nz + 1,)), dma((nz + 1,)), dma((nz, 2, 2)), dma((nz, 2)),
            dma((nz, hp)), dma((nz, hp)), dma((nz, hp)), dma((nz + 1, hp)),
            dma((n_col,)), dma((n_row, kr)), dma((n_row,)), dma((n_row,)),
        ],
        compiler_params=pltpu.CompilerParams(
            collective_id=0, has_side_effects=True, vmem_limit_bytes=60 * 1024 * 1024
        ),
    )(members, ancestor_inv, lower_panel, upper_panel, pivot_inv)


def solution(mesh):
    return jax.shard_map(
        body,
        mesh=mesh,
        in_specs=(
            P("row", "col", None, None),
            P("row", "col", None, None),
            P("col", "row", None, None),
            P("col", None, None),
            P(),
        ),
        out_specs=(P("col", "row", None, None), P("row", "col", None, None), P("col", None, None)),
        check_vma=False,
    )
```

time: 342 us -> 119 us (0.35)
  waiting for transfers between devices: 283 us -> 0 us
  Pallas kernels: 0 us -> 113 us
  matrix products: 20.3 us -> 0 us
  between operations: 13.9 us -> 0.64 us
  other arithmetic: 6.15 us -> 0 us
  blocking collectives: 6.15 us -> 0 us
  local copies, waits for them, and re-layouts: 9.86 us -> 5.4 us
    reduce_scatter x3 -> x0, waiting for transfers between devices: 204 us -> none  [the longest x1 139 us: body(): lax.psum_scatter(lower_part, 'col', scatter_dimension=0, tiled=True)]
    pallas_call x0 -> x1, Pallas kernels: none -> 113 us  [body(): pl.pallas_call(functools.partial(kernel, n_row, n_col, nq, hp), out_shape...]
    all_gather x2 -> x0, waiting for transfers between devices: 78.4 us -> none  [the longest x1 64.2 us: body(): lax.all_gather(upper_panel, 'col', axis=0, tiled=True)]
    dot_general x3 -> x0, matrix products: 20.3 us -> none  [the longest x1 9.72 us: body(): jnp.einsum('kiab,kijbc->kjac', masked, pairs_here, preferred_element_type...]
    gather x1 -> x0, local copies, waits for them, and re-layouts: 7.78 us -> none  [body(): jnp.take(ancestor_inv.reshape(row_blocks * col_blocks, side, side), flat_...]
    all_gather x1 -> x0, blocking collectives: 6.15 us -> none  [body(): lax.all_gather(diag_band.astype(jnp.bfloat16), 'row', axis=1, tiled=True)]
    convert_element_type x3 -> x0, other arithmetic: 3.46 us -> none  [the longest x1 1.31 us: body(): lower_inv = (-lower_sum).astype(jnp.bfloat16)]
    unnamed x9 -> x3, local copies, waits for them, and re-layouts: 1.96 us -> 5.4 us
  transfers between devices with their start and end apart: 5 -> 0, of which waited for: 5 -> 0; matrix products, arithmetic and copies ran while one was open for 10% -> 0% of each run, Pallas kernels for 0% -> 0%
where the time goes in v1:
time: 119 us
  Pallas kernels  113 us (95%)
  local copies, waits for them, and re-layouts  5.4 us (5%)
    pallas_call x1, Pallas kernels, body(): pl.pallas_call(functools.partial(kernel, n_row, n_col, nq, hp), out_shape...  113 us
    unnamed x3, local copies, waits for them, and re-layouts  5.4 us

profile of v1, /device:TPU:27, one launch (start us, length us, event | category | flops | bytes accessed | tf_op | source)
XLA Modules:
  0.0 118.7 jit_solution(16790467979100760275)
XLA Ops:
  0.6 112.7 %shard_map.76 = (bf16[1,4,256,256]{3,2,1,0:T(8,128)(2,1)}, bf16[2,2,256,256]{3,2,1,0:T(8,128)(2,1)}, f32[1,256,256]{2,1,0:T(8,128)}) custom-call(s32[8,16]{1,0:T(8,128)} %mem.1, bf16[8,4,256,256]{3,2,1,0:T(8,128)(2,1)} %anc.1, bf16[2,2,256,256]{3,2,1,0:T(8,128)(2,1)} %low.1, bf16[1,4,256,256]{3,2,1,0:T(8,128)(2,1)} %upp.1, f32[1,256,256]{2,1,0:T(8,128)} %piv.1), custom_call_target="tpu_custom_call" | custom-call | tf_op jit(solution)/shard_map/pallas_call | solution.py:449
  113.3 1.9 %copy.11 = bf16[1,4,256,256]{3,2,1,0:T(8,128)(2,1)} copy(bf16[1,4,256,256]{3,2,1,0:T(8,128)(2,1)} %get-tuple-element.6) | data formatting | bytes 1048576
  115.2 1.9 %copy.12 = bf16[2,2,256,256]{3,2,1,0:T(8,128)(2,1)} copy(bf16[2,2,256,256]{3,2,1,0:T(8,128)(2,1)} %get-tuple-element.7) | data formatting | bytes 1048576
  117.1 1.7 %copy.13 = f32[1,256,256]{2,1,0:T(8,128)} copy(f32[1,256,256]{2,1,0:T(8,128)} %get-tuple-element.8) | data formatting | bytes 524288

commit v2 on v1

--- a/solution.py
+++ b/solution.py
@@ -125,6 +125,11 @@
     def d_got(r2):
         return remote(ds, dr.at[r2], d_s.at[r2], d_r.at[r2], row=r2)
 
+    def d_relay(x2):
+        r2 = x2 * CORES + core
+        blk = dr.at[r2]
+        return remote(blk, blk, d_s.at[x2 * CORES + 1 - core], d_r.at[r2], row=partner)
+
     def each_dir(fn):
         @pl.when(z > 0)
         def _():
@@ -194,6 +199,18 @@
 
         lax.fori_loop(0, kr, one, 0)
 
+    def target(t):
+        x2 = (x + t // CORES) % nx
+        q = t % CORES
+        return x2 * CORES + jnp.where(2 * x2 >= nx, CORES - 1 - q, q)
+
+    def both_groups(x2):
+        def one(q, _):
+            lower_group(x2 * CORES + jnp.where(2 * x2 >= nx, CORES - 1 - q, q))
+            return 0
+
+        lax.fori_loop(0, CORES, one, 0)
+
     l_own(partner).start()
     for dx in range(1, nx):
         l_own(((x + dx) % nx) * CORES + core).start()
@@ -202,9 +219,8 @@
 
     ca.wait()
     cl.wait()
-    lower_group(row)
     l_recv(partner).wait_recv()
-    lower_group(partner)
+    both_groups(x)
 
     uy_got(0, z).wait_recv()
     each_dir(lambda up: uz(z, 1, up).start())
@@ -241,9 +257,8 @@
     by_side(1, take)
 
     def late(x2):
-        lower_group(x2 * CORES + core)
         l_recv(x2 * CORES + 1 - core).wait_recv()
-        lower_group(x2 * CORES + 1 - core)
+        both_groups(x2)
 
     others(late)
     uy_own(1).start()
@@ -311,19 +326,49 @@
             go(False)
 
     def chain(t):
-        band_sum((CORES * x + t) % nz, t)
+        band_sum(target(t), t)
 
     near(1)
-    chain(0)
-    for d in range(2, nz):
+    edge = jnp.logical_or(z == 0, z == nz - 1)
+
+    def take_pass(d):
         by_side(d, take)
         by_side(d, lambda zs, up: uy_pass(zs).start())
         near(d)
-        chain(d - 1)
+
+    def chains(t, _):
+        chain(t)
+        return 0
+
+    @pl.when(edge)
+    def _():
+        lax.fori_loop(0, CORES, chains, 0)
+
+    @pl.when(jnp.logical_not(edge))
+    def _():
+        def one(d, _):
+            take_pass(d)
+            return 0
+
+        lax.fori_loop(2, nz - 1, one, 0)
+        lax.fori_loop(0, CORES, chains, 0)
+
+    @pl.when(edge)
+    def _():
+        def one(d, _):
+            take_pass(d)
+            chain(CORES + d - 2)
+            return 0
+
+        lax.fori_loop(2, nz, one, 0)
+
+    @pl.when(jnp.logical_not(edge))
+    def _():
+        lax.fori_loop(CORES, nz, chains, 0)
+
     uy_got(1, z).wait_recv()
     upper_part(yp)
     far(1)
-    chain(nz - 1)
 
     def final(h, _):
         part = pl.ds(h * hb, hb)
@@ -353,15 +398,28 @@
         tot = t if tot is None else tot + t
     dacc[...] = tot
     ds[...] = tot.astype(BF)
-    for dx in range(1, n_row):
-        d_copy((row + dx) % n_row).start()
+    others(lambda x2: d_copy(x2 * CORES + core).start())
+    d_copy(partner).start()
 
     lax.fori_loop(2, nz, lambda d, _: (far(d), 0)[1], 0)
 
-    for dx in range(1, n_row):
-        r2 = (row + dx) % n_row
-        d_got(r2).wait_recv()
+    def d_pass(x2):
+        d_got(x2 * CORES + core).wait_recv()
+        d_relay(x2).start()
+
+    def d_add(r2):
         dacc[...] = dacc[...] + dr[r2].astype(F32)
+
+    others(d_pass)
+    d_got(partner).wait_recv()
+    d_add(partner)
+
+    def d_add_chip(x2):
+        d_add(x2 * CORES + core)
+        d_got(x2 * CORES + 1 - core).wait_recv()
+        d_add(x2 * CORES + 1 - core)
+
+    others(d_add_chip)
     diag_out[0] = piv[0] - dacc[...]
 
     for p in range(kr):
@@ -426,8 +484,18 @@
         return 0
 
     lax.fori_loop(0, n_col, parts_done, 0)
-    for dx in range(1, n_row):
-        d_copy((row + dx) % n_row).wait_send()
+    d_copy(partner).wait_send()
+
+    def d_done(x2):
+        d_copy(x2 * CORES + core).wait_send()
+        d_relay(x2).wait_send()
+
+    others(d_done)
+
+
+def hand_over(*refs):
+    for src, dst in zip(refs[:3], refs[3:]):
+        dst[...] = src[...]
 
 
 def body(ancestor_inv, lower_panel, upper_panel, pivot_inv, members):
@@ -441,12 +509,14 @@
     nz = n_col // NY
     assert per_col == 1 and level == n_col and kr == NY and nz == n_row
     hp = 2
-    nq = rs // 4
+    nq = rs // 2
     blk = (side, side)
     dma = pltpu.SemaphoreType.DMA
     vmem = pl.BlockSpec(memory_space=pltpu.VMEM)
     hbm = pl.BlockSpec(memory_space=pltpu.HBM)
-    return pl.pallas_call(
+    held = rb * cb + 3 * level * cs + 2 * n_col * rs + (2 * nz + 1) * rs + n_row * (kr * cs + 1)
+    limit = 2 * side * side * (held + 32)
+    outs = pl.pallas_call(
         functools.partial(kernel, n_row, n_col, nq, hp),
         out_shape=(
             jax.ShapeDtypeStruct((per_col, rs) + blk, BF),
@@ -477,6 +547,12 @@
             collective_id=0, has_side_effects=True, vmem_limit_bytes=60 * 1024 * 1024
         ),
     )(members, ancestor_inv, lower_panel, upper_panel, pivot_inv)
+    return pl.pallas_call(
+        hand_over,
+        out_shape=tuple(jax.ShapeDtypeStruct(o.shape, o.dtype) for o in outs),
+        in_specs=[vmem] * 3,
+        out_specs=(vmem,) * 3,
+    )(*outs)
 
 
 def solution(mesh):

time: 119 us -> 93.8 us (0.79)
  the two profiles are of different devices: /device:TPU:27 before, /device:TPU:11 now
where the time goes in v2:
time: 93.8 us; the launch traced here: 93.6 us
  Pallas kernels  93 us (99%)
    pallas_call x1, Pallas kernels, body(): pl.pallas_call(functools.partial(kernel, n_row, n_col, nq, hp), out_shape...  90.6 us
    pallas_call x1, Pallas kernels, body(): pl.pallas_call(hand_over, out_shape=tuple((jax.ShapeDtypeStruct(o.shape,...  2.35 us

profile of v2, /device:TPU:11, one launch (start us, length us, event | category | flops | bytes accessed | tf_op | source)
XLA Modules:
  0.0 93.6 jit_solution(12596841127034035089)
XLA Ops:
  0.6 90.6 %shard_map.76 = (bf16[1,4,256,256]{3,2,1,0:T(8,128)(2,1)}, bf16[2,2,256,256]{3,2,1,0:T(8,128)(2,1)}, f32[1,256,256]{2,1,0:T(8,128)}) custom-call(s32[8,16]{1,0:T(8,128)} %mem.1, bf16[8,4,256,256]{3,2,1,0:T(8,128)(2,1)} %anc.1, bf16[2,2,256,256]{3,2,1,0:T(8,128)(2,1)} %low.1, bf16[1,4,256,256]{3,2,1,0:T(8,128)(2,1)} %upp.1, f32[1,256,256]{2,1,0:T(8,128)} %piv.1), custom_call_target="tpu_custom_call" | custom-call | tf_op jit(solution)/shard_map/pallas_call | solution.py:519
  91.3 2.3 %shard_map.77 = (bf16[1,4,256,256]{3,2,1,0:T(8,128)(2,1)}, bf16[2,2,256,256]{3,2,1,0:T(8,128)(2,1)}, f32[1,256,256]{2,1,0:T(8,128)}) custom-call(bf16[1,4,256,256]{3,2,1,0:T(8,128)(2,1)} %get-tuple-element.6.refs_0_, bf16[2,2,256,256]{3,2,1,0:T(8,128)(2,1)} %get-tuple-element.7.refs_1_, f32[1,256,256]{2,1,0:T(8,128)} %get-tuple-element.8.refs_2_), custom_call_target="tpu_custom_call" | custom-call | tf_op jit(solution)/shard_map/pallas_call | solution.py:550
